TPU v7x, 32 devices: a whole 2x2x4 slice. The times are simulated.
32 devices in a mesh: groups: 2 (over y), seq: 4 (over z), section: 2 (over x), kv: 2 (over core).
Axes of the slice: x: 2, y: 2, z: 4, core: 2. Of those that a mesh axis runs over, the one named last changes fastest.
Arguments:
- queries: bfloat16 [4, 1024, 2560], P(('groups', 'section'), 'seq', 'kv'), parts along dimension 0, may hold values from -128 to 128
- key_rows: bfloat16 [4, 1024, 512], P(('groups', 'section'), 'seq', 'kv'), parts along dimension 0, may hold values from -4 to 4
- values: bfloat16 [4, 1024, 512], P(('groups', 'section'), 'seq', 'kv'), parts along dimension 0, may hold values from -6 to 6
- lengths: int32 [4, 3], P(('groups', 'section')), parts along dimension 0, may hold values from 1 to 32, 64 in all within a row
- block_order: int32 [4, 4], P(('groups', 'section')), parts along dimension 0, may hold values from 0 to 3, each once within a row
- page_owner: int32 [4, 64, 1], P(('groups', 'section')), parts along dimension 0, may hold values from 0 to 3; in each aligned block of 16 rows (0 to 15, 16 to 31, ..., all dimensions but the last counted through in order) at most 8 rows name the same one
Outputs:
- handed: bfloat16 [4, 1024, 2560], P(('groups', 'section'), 'seq', 'kv'), parts along dimension 0
- cache_keys: bfloat16 [4, 4, 512, 512], P(('groups', 'section'), 'seq', None, 'kv'), parts along dimension 0
- cache_values: bfloat16 [4, 4, 512, 512], P(('groups', 'section'), 'seq', None, 'kv'), parts along dimension 0
There are 2 independent parts, one for each index of `groups`. A program takes and returns all parts, laid end to end along the dimension named above; each array names one. Nothing has to cross between parts.
Inputs may be any that keep to these rules, and one draw needn't show every extreme that they name: `lengths`: lengths sum to 64; the longest request has exactly 32 pages. `block_order`: each row is a permutation of the seq indices. `page_owner`: among the 16 pages of one aligned device block, no owner is named more than 8 times.
All inputs are finite; a program needn't handle non-finite values.
Results may differ from a plain program's by a relative error of at most 0.0038.
Values may be sent and summed in bfloat16 or wider, within the bound.
A program may use at most 64 MiB of HBM per device.

v0:
```python
import functools
import math

import jax
import jax.numpy as jnp
from jax import lax
from jax.experimental import pallas as pl
from jax.experimental.pallas import tpu as pltpu
from jax.sharding import PartitionSpec as P

HEAD = 128
PAGE = 16
NEG = -1e30
MESH = pl.DeviceIdType.MESH


def greet(barrier, peer):
    pl.semaphore_signal(barrier, inc=1, device_id=peer, device_id_type=MESH)


def kernel(
    dims,
    lengths,
    order,
    owner,
    q_hbm,
    k_hbm,
    v_hbm,
    handed,
    ck_hbm,
    cv_hbm,
    q,
    kall,
    vall,
    bias,
    ctx,
    ck,
    cv,
    in_sem,
    send_sem,
    recv_sem,
    hand_send,
    hand_recv,
    out_sem,
):
    n, sections, tok, kv_heads, width, slots = dims
    pages = tok // PAGE
    me = lax.axis_index("seq")
    sec = lax.axis_index("section")
    right, left = me + 1, me - 1
    onward, before = lax.rem(sec + 1, sections), lax.rem(sec + sections - 1, sections)
    half = tok // 2

    def block(ref, g, index):
        rows = pl.ds(pl.multiple_of(index * tok, tok), tok)
        return ref.at[g, rows, pl.ds(0, HEAD)]

    loads = []
    for g in range(kv_heads):
        for t, (src, dst) in enumerate(((k_hbm, kall), (v_hbm, vall))):
            load = pltpu.make_async_copy(
                src.at[0, :, pl.ds(g * HEAD, HEAD)], block(dst, g, me), in_sem.at[2 * g + t]
            )
            load.start()
            loads.append(load)
    q_load = pltpu.make_async_copy(q_hbm.at[0], q, in_sem.at[2 * kv_heads])
    q_load.start()

    barrier = pltpu.get_barrier_semaphore()
    others = []
    if sections > 1:
        others.append({"section": onward})
    if sections > 2:
        others.append({"section": before})
    pl.when(me < n - 1)(lambda: greet(barrier, {"seq": right}))
    pl.when(me > 0)(lambda: greet(barrier, {"seq": left}))
    for peer in others:
        greet(barrier, peer)
    beside = jnp.where(me < n - 1, 1, 0) + jnp.where(me > 0, 1, 0)
    pl.semaphore_wait(barrier, beside + len(others))

    def sends(way, d):
        return (me < n - 1) & (me >= d - 1) if way == 0 else (me > 0) & (me <= n - d)

    def takes(way, d):
        return me >= d if way == 0 else me + d <= n - 1

    def line(way, g, d, t, arriving):
        shift = d if arriving else d - 1
        ref = block((kall, vall)[t], g, me - shift if way == 0 else me + shift)
        return pltpu.make_async_remote_copy(
            src_ref=ref,
            dst_ref=ref,
            send_sem=send_sem.at[way, g, d - 1, t],
            recv_sem=recv_sem.at[way, g, d - 1, t],
            device_id={"seq": right if way == 0 else left},
            device_id_type=MESH,
        )

    def start(g, ts=(0, 1)):
        for t in ts:
            for way in range(2):
                pl.when(sends(way, 1))(lambda: line(way, g, 1, t, False).start())

    def pass_on(g, d):
        for t in range(2):
            for way in range(2):

                @pl.when(sends(way, d + 1))
                def _():
                    line(way, g, d, t, True).wait_recv()
                    line(way, g, d + 1, t, False).start()

    def settle(g):
        for d in range(1, n):
            for t in range(2):
                for way in range(2):
                    ends = takes(way, d) & jnp.logical_not(sends(way, d + 1))
                    pl.when(ends)(lambda: line(way, g, d, t, True).wait_recv())

    loads[0].wait()
    loads[1].wait()
    start(0)
    for load in loads[2:]:
        load.wait()
    for g in range(1, kv_heads):
        start(g, (0,))

    vall[:, :, HEAD:] = jnp.ones((kv_heads, n * tok, HEAD), vall.dtype)
    begins = [0]
    for r in range(lengths.shape[1] - 1):
        begins.append(begins[-1] + lengths[0, r])

    def request(position):
        page = position // PAGE
        total = jnp.zeros_like(position)
        for begin in begins[1:]:
            total = total + (page >= begin).astype(jnp.int32)
        return total

    q_pos = order[0, me] * tok + lax.broadcasted_iota(jnp.int32, (tok, 1), 0)
    q_req = request(q_pos)

    def mask(i, _):
        k_pos = order[0, i] * tok + lax.broadcasted_iota(jnp.int32, (1, tok), 1)
        allowed = (request(k_pos) == q_req) & (k_pos <= q_pos)
        bias[:, pl.ds(pl.multiple_of(i * tok, tok), tok)] = jnp.where(allowed, 0.0, NEG)
        return 0

    lax.fori_loop(0, n, mask, 0)
    q_load.wait()

    for d in range(1, n - 1):
        pass_on(0, d)
    for g in range(1, kv_heads):
        start(g, (1,))
    settle(0)

    factor = math.log2(math.e) / math.sqrt(HEAD)

    def hand(h):
        cols = pl.ds(pl.multiple_of(h * HEAD, HEAD), HEAD)
        return pltpu.make_async_remote_copy(
            src_ref=ctx.at[:, cols],
            dst_ref=handed.at[0, :, cols],
            send_sem=hand_send.at[h],
            recv_sem=hand_recv.at[h],
            device_id={"section": onward},
            device_id_type=MESH,
        )

    def heads(g, low, high):
        def one(j, _):
            h = g * width + j
            cols = pl.ds(pl.multiple_of(h * HEAD, HEAD), HEAD)
            for part in range(2):
                rows = pl.ds(part * half, half)
                score = lax.dot_general(
                    q[rows, cols],
                    kall[g],
                    (((1,), (1,)), ((), ())),
                    preferred_element_type=jnp.float32,
                )
                score = score * factor + bias[rows, :]
                top = jnp.max(score, axis=1, keepdims=True)
                weight = jnp.exp2(score - top).astype(jnp.bfloat16)
                mixed = jnp.dot(weight, vall[g], preferred_element_type=jnp.float32)
                ctx[rows, cols] = (mixed[:, :HEAD] / mixed[:, HEAD:]).astype(ctx.dtype)
            hand(h).start()
            return 0

        lax.fori_loop(low, high, one, 0)

    for g in range(kv_heads):
        last = g + 1 == kv_heads
        for low in range(0, width, 2):
            heads(g, low, min(low + 2, width))
            d = low // 2 + 1
            if not last and d < n - 1 and low + 2 < width:
                pass_on(g + 1, d)
        if not last:
            for d in range((width - 1) // 2 + 1, n - 1):
                pass_on(g + 1, d)
            settle(g + 1)

    taken = slots * PAGE
    lane_page = lax.broadcasted_iota(jnp.int32, (1, tok), 1) // PAGE
    lane_token = lax.broadcasted_iota(jnp.int32, (1, tok), 1) % PAGE

    def pick(i, _):
        base = order[0, i] * pages
        target = jnp.full((1, tok), -1, jnp.int32)
        rank = jnp.int32(0)
        for p in range(pages):
            mine = owner[0, base + p] == me
            target = jnp.where(lane_page == p, jnp.where(mine, rank * PAGE, -taken), target)
            rank = rank + mine.astype(jnp.int32)
        target = target + lane_token
        select = (lax.broadcasted_iota(jnp.int32, (taken, tok), 0) == target).astype(jnp.bfloat16)
        rows = pl.ds(pl.multiple_of(i * tok, tok), tok)
        outs = pl.ds(pl.multiple_of(i * taken, taken), taken)
        for g in range(kv_heads):
            cols = pl.ds(g * HEAD, HEAD)
            for dst, src in ((ck, kall), (cv, vall)):
                dst[outs, cols] = jnp.dot(
                    select, src[g, rows, :HEAD], preferred_element_type=jnp.float32
                ).astype(dst.dtype)
        return 0

    lax.fori_loop(0, n, pick, 0)
    writes = [
        pltpu.make_async_copy(ck, ck_hbm.at[0, 0], out_sem.at[0]),
        pltpu.make_async_copy(cv, cv_hbm.at[0, 0], out_sem.at[1]),
    ]
    for write in writes:
        write.start()

    for g in range(kv_heads):
        for d in range(1, n):
            for t in range(2):
                for way in range(2):
                    pl.when(sends(way, d))(lambda: line(way, g, d, t, False).wait_send())

    def finish(h, _):
        copy = hand(h)
        copy.wait_send()
        copy.wait_recv()
        return 0

    lax.fori_loop(0, kv_heads * width, finish, 0)
    for write in writes:
        write.wait()


def body(queries, key_rows, values, lengths, block_order, page_owner):
    n, sections = lax.axis_size("seq"), lax.axis_size("section")
    tok = key_rows.shape[1]
    kv_heads = key_rows.shape[2] // HEAD
    heads = queries.shape[2] // HEAD
    slots = max(2, 2 * (tok // PAGE) // n)
    dims = (n, sections, tok, kv_heads, heads // kv_heads, slots)
    steps = max(n - 1, 1)
    taken = n * slots * PAGE
    dtype = queries.dtype
    smem = pl.BlockSpec(memory_space=pltpu.SMEM)
    hbm = pl.BlockSpec(memory_space=pltpu.HBM)
    return pl.pallas_call(
        functools.partial(kernel, dims),
        out_shape=(
            jax.ShapeDtypeStruct(queries.shape, dtype),
            jax.ShapeDtypeStruct((1, 1, taken, key_rows.shape[2]), dtype),
            jax.ShapeDtypeStruct((1, 1, taken, key_rows.shape[2]), dtype),
        ),
        in_specs=[smem, smem, smem, hbm, hbm, hbm],
        out_specs=(hbm, hbm, hbm),
        scratch_shapes=[
            pltpu.VMEM((tok, heads * HEAD), dtype),
            pltpu.VMEM((kv_heads, n * tok, HEAD), dtype),
            pltpu.VMEM((kv_heads, n * tok, 2 * HEAD), dtype),
            pltpu.VMEM((tok, n * tok), jnp.float32),
            pltpu.VMEM((tok, heads * HEAD), dtype),
            pltpu.VMEM((taken, kv_heads * HEAD), dtype),
            pltpu.VMEM((taken, kv_heads * HEAD), dtype),
            pltpu.SemaphoreType.DMA((2 * kv_heads + 1,)),
            pltpu.SemaphoreType.DMA((2, kv_heads, steps, 2)),
            pltpu.SemaphoreType.DMA((2, kv_heads, steps, 2)),
            pltpu.SemaphoreType.DMA((heads,)),
            pltpu.SemaphoreType.DMA((heads,)),
            pltpu.SemaphoreType.DMA((2,)),
        ],
        compiler_params=pltpu.CompilerParams(
            collective_id=0, has_side_effects=True
        ),
    )(
        lengths,
        block_order,
        page_owner.reshape(page_owner.shape[:2]),
        queries,
        key_rows,
        values,
    )


def solution(mesh):
    in_specs = (
        P(("groups", "section"), "seq", "kv"),
        P(("groups", "section"), "seq", "kv"),
        P(("groups", "section"), "seq", "kv"),
        P(("groups", "section"), None),
        P(("groups", "section"), None),
        P(("groups", "section"), None, None),
    )
    out_specs = (
        P(("groups", "section"), "seq", "kv"),
        P(("groups", "section"), "seq", None, "kv"),
        P(("groups", "section"), "seq", None, "kv"),
    )
    return jax.shard_map(body, mesh=mesh, in_specs=in_specs, out_specs=out_specs, check_vma=False)
```

profile of v0, /device:TPU:0, one launch (start us, length us, event | category | flops | bytes accessed | tf_op | source)
XLA Modules:
  0.0 37.9 jit_solution(11489661495833706588)
XLA Ops:
  0.6 33.4 %shard_map.85 = (bf16[1,256,1280]{2,1,0:T(8,128)(2,1)}, bf16[1,1,512,256]{3,2,1,0:T(8,128)(2,1)}, bf16[1,1,512,256]{3,2,1,0:T(8,128)(2,1)}) custom-call(s32[1,3]{1,0:T(1,128)} %lengths.1, s32[1,4]{1,0:T(1,128)} %order.1, s32[1,64]{1,0:T(1,128)} %bitcast.1, bf16[1,256,1280]{2,1,0:T(8,128)(2,1)} %q_hbm.1, bf16[1,256,256]{2,1,0:T(8,128)(2,1)} %k_hbm.1, ...), custom_call_target="tpu_custom_call" | custom-call | tf_op jit(solution)/shard_map/pallas_call | solution.py:267
  34.1 0.0 copy-start.1
  34.1 2.0 %copy.12 = bf16[1,256,1280]{2,1,0:T(8,128)(2,1)} copy(bf16[1,256,1280]{2,1,0:T(8,128)(2,1)} %get-tuple-element.6) | data formatting | bytes 1310720
  36.1 0.0 copy-done.1
  36.1 0.0 copy-start
  36.1 0.7 %copy.13 = bf16[1,1,512,256]{3,2,1,0:T(8,128)(2,1)} copy(bf16[1,1,512,256]{3,2,1,0:T(8,128)(2,1)S(1)} %copy-done.1) | data formatting | bytes 524288
  36.8 0.3 copy-done
  37.1 0.7 %copy.14 = bf16[1,1,512,256]{3,2,1,0:T(8,128)(2,1)} copy(bf16[1,1,512,256]{3,2,1,0:T(8,128)(2,1)S(1)} %copy-done) | data formatting | bytes 524288
Async XLA Ops:
  34.1 2.0 %copy-start.1 = (bf16[1,1,512,256]{3,2,1,0:T(8,128)(2,1)S(1)}, bf16[1,1,512,256]{3,2,1,0:T(8,128)(2,1)}, u32[]{:S(2)}) copy-start(bf16[1,1,512,256]{3,2,1,0:T(8,128)(2,1)} %get-tuple-element.7) | copy-start | bytes 786436
  36.1 1.0 %copy-start = (bf16[1,1,512,256]{3,2,1,0:T(8,128)(2,1)S(1)}, bf16[1,1,512,256]{3,2,1,0:T(8,128)(2,1)}, u32[]{:S(2)}) copy-start(bf16[1,1,512,256]{3,2,1,0:T(8,128)(2,1)} %get-tuple-element.8) | copy-start | bytes 786436
where the time goes:
time: 38 us; the launch traced here: 37.9 us
  Pallas kernels  33.4 us (88%)
  local copies, waits for them, and re-layouts  3.76 us (10%)
  between operations  0.65 us (2%)
    pallas_call x1, Pallas kernels, body(): pl.pallas_call(functools.partial(kernel, dims), out_shape=(jax.ShapeDtype...  33.4 us
    unnamed x7, local copies, waits for them, and re-layouts  3.76 us

commit v1 on v0

--- a/solution.py
+++ b/solution.py
@@ -20,28 +20,29 @@
 
 def kernel(
     dims,
-    lengths,
-    order,
-    owner,
+    lengths_hbm,
+    order_hbm,
+    owner_hbm,
     q_hbm,
     k_hbm,
     v_hbm,
     handed,
-    ck_hbm,
-    cv_hbm,
+    ck,
+    cv,
     q,
     kall,
     vall,
     bias,
     ctx,
-    ck,
-    cv,
+    lengths,
+    order,
+    owner,
+    meta_sem,
     in_sem,
     send_sem,
     recv_sem,
     hand_send,
     hand_recv,
-    out_sem,
 ):
     n, sections, tok, kv_heads, width, slots = dims
     pages = tok // PAGE
@@ -63,6 +64,10 @@
             )
             load.start()
             loads.append(load)
+    metas = []
+    for src, dst in ((lengths_hbm, lengths), (order_hbm, order), (owner_hbm, owner)):
+        metas.append(pltpu.make_async_copy(src, dst, meta_sem.at[len(metas)]))
+        metas[-1].start()
     q_load = pltpu.make_async_copy(q_hbm.at[0], q, in_sem.at[2 * kv_heads])
     q_load.start()
 
@@ -127,6 +132,8 @@
         start(g, (0,))
 
     vall[:, :, HEAD:] = jnp.ones((kv_heads, n * tok, HEAD), vall.dtype)
+    for meta in metas:
+        meta.wait()
     begins = [0]
     for r in range(lengths.shape[1] - 1):
         begins.append(begins[-1] + lengths[0, r])
@@ -162,7 +169,7 @@
         cols = pl.ds(pl.multiple_of(h * HEAD, HEAD), HEAD)
         return pltpu.make_async_remote_copy(
             src_ref=ctx.at[:, cols],
-            dst_ref=handed.at[0, :, cols],
+            dst_ref=handed.at[:, cols],
             send_sem=hand_send.at[h],
             recv_sem=hand_recv.at[h],
             device_id={"section": onward},
@@ -228,13 +235,6 @@
         return 0
 
     lax.fori_loop(0, n, pick, 0)
-    writes = [
-        pltpu.make_async_copy(ck, ck_hbm.at[0, 0], out_sem.at[0]),
-        pltpu.make_async_copy(cv, cv_hbm.at[0, 0], out_sem.at[1]),
-    ]
-    for write in writes:
-        write.start()
-
     for g in range(kv_heads):
         for d in range(1, n):
             for t in range(2):
@@ -248,8 +248,22 @@
         return 0
 
     lax.fori_loop(0, kv_heads * width, finish, 0)
-    for write in writes:
-        write.wait()
+
+
+def store(handed_v, ck_v, cv_v, handed, ck, cv, sem):
+    copies = []
+    for src, dst in ((handed_v, handed), (ck_v, ck), (cv_v, cv)):
+        rows = src.shape[0] // 2
+        view = dst.at[0] if dst.ndim == 3 else dst.at[0, 0]
+        for part in range(2):
+            piece = pl.ds(part * rows, rows)
+            copies.append(
+                pltpu.make_async_copy(src.at[piece], view.at[piece], sem.at[len(copies)])
+            )
+    for copy in copies:
+        copy.start()
+    for copy in copies:
+        copy.wait()
 
 
 def body(queries, key_rows, values, lengths, block_order, page_owner):
@@ -262,43 +276,54 @@
     steps = max(n - 1, 1)
     taken = n * slots * PAGE
     dtype = queries.dtype
-    smem = pl.BlockSpec(memory_space=pltpu.SMEM)
     hbm = pl.BlockSpec(memory_space=pltpu.HBM)
-    return pl.pallas_call(
+    metas = lengths, block_order, page_owner.reshape(page_owner.shape[:2])
+    vmem = pl.BlockSpec(memory_space=pltpu.VMEM)
+    width = key_rows.shape[2]
+    held = pl.pallas_call(
         functools.partial(kernel, dims),
         out_shape=(
-            jax.ShapeDtypeStruct(queries.shape, dtype),
-            jax.ShapeDtypeStruct((1, 1, taken, key_rows.shape[2]), dtype),
-            jax.ShapeDtypeStruct((1, 1, taken, key_rows.shape[2]), dtype),
+            pltpu.VMEM(queries.shape[1:], dtype),
+            pltpu.VMEM((taken, width), dtype),
+            pltpu.VMEM((taken, width), dtype),
         ),
-        in_specs=[smem, smem, smem, hbm, hbm, hbm],
-        out_specs=(hbm, hbm, hbm),
+        in_specs=[hbm] * 6,
+        out_specs=(vmem, vmem, vmem),
         scratch_shapes=[
             pltpu.VMEM((tok, heads * HEAD), dtype),
             pltpu.VMEM((kv_heads, n * tok, HEAD), dtype),
             pltpu.VMEM((kv_heads, n * tok, 2 * HEAD), dtype),
             pltpu.VMEM((tok, n * tok), jnp.float32),
             pltpu.VMEM((tok, heads * HEAD), dtype),
-            pltpu.VMEM((taken, kv_heads * HEAD), dtype),
-            pltpu.VMEM((taken, kv_heads * HEAD), dtype),
+            *(pltpu.SMEM(x.shape, x.dtype) for x in metas),
+            pltpu.SemaphoreType.DMA((3,)),
             pltpu.SemaphoreType.DMA((2 * kv_heads + 1,)),
             pltpu.SemaphoreType.DMA((2, kv_heads, steps, 2)),
             pltpu.SemaphoreType.DMA((2, kv_heads, steps, 2)),
             pltpu.SemaphoreType.DMA((heads,)),
             pltpu.SemaphoreType.DMA((heads,)),
-            pltpu.SemaphoreType.DMA((2,)),
         ],
         compiler_params=pltpu.CompilerParams(
-            collective_id=0, has_side_effects=True
+            collective_id=0, has_side_effects=True, vmem_limit_bytes=48 << 20
         ),
     )(
-        lengths,
-        block_order,
-        page_owner.reshape(page_owner.shape[:2]),
-        queries,
-        key_rows,
-        values,
+        *(
+            pltpu.with_memory_space_constraint(x, pltpu.HBM)
+            for x in (*metas, queries, key_rows, values)
+        ),
     )
+    return pl.pallas_call(
+        store,
+        out_shape=(
+            jax.ShapeDtypeStruct(queries.shape, dtype),
+            jax.ShapeDtypeStruct((1, 1, taken, width), dtype),
+            jax.ShapeDtypeStruct((1, 1, taken, width), dtype),
+        ),
+        in_specs=[vmem, vmem, vmem],
+        out_specs=(hbm, hbm, hbm),
+        scratch_shapes=[pltpu.SemaphoreType.DMA((6,))],
+        compiler_params=pltpu.CompilerParams(vmem_limit_bytes=8 << 20),
+    )(*(pltpu.with_memory_space_constraint(x, pltpu.VMEM) for x in held))
 
 
 def solution(mesh):

time: 38 us -> 34.4 us (0.905)
  local copies, waits for them, and re-layouts: 3.76 us -> 0 us
    unnamed x7 -> x0, local copies, waits for them, and re-layouts: 3.76 us -> none
    pallas_call x1 -> x2, Pallas kernels: 33.4 us -> 33.6 us  [the longest x1 32.6 us: body(): pl.pallas_call(functools.partial(kernel, dims), out_shape=(pltpu.VMEM(que...]
where the time goes in v1:
time: 34.4 us; the launch traced here: 34.3 us
  Pallas kernels  33.6 us (98%)
  between operations  0.64 us (2%)
    pallas_call x1, Pallas kernels, body(): pl.pallas_call(functools.partial(kernel, dims), out_shape=(pltpu.VMEM(que...  32.6 us
    pallas_call x1, Pallas kernels, body(): pl.pallas_call(store, out_shape=(jax.ShapeDtypeStruct(queries.shape, dtyp...  1.06 us

profile of v1, /device:TPU:0, one launch (start us, length us, event | category | flops | bytes accessed | tf_op | source)
XLA Modules:
  0.0 34.3 jit_solution(13325774000247071048)
XLA Ops:
  0.6 32.6 %shard_map.85 = (bf16[256,1280]{1,0:T(8,128)(2,1)S(1)}, bf16[512,256]{1,0:T(8,128)(2,1)S(1)}, bf16[512,256]{1,0:T(8,128)(2,1)S(1)}) custom-call(s32[1,3]{1,0:T(1,128)} %lengths_hbm.1, s32[1,4]{1,0:T(1,128)} %order_hbm.1, s32[1,64]{1,0:T(1,128)} %bitcast.1, bf16[1,256,1280]{2,1,0:T(8,128)(2,1)} %q_hbm.1, bf16[1,256,256]{2,1,0:T(8,128)(2,1)} %k_hbm.1, ...), custom_call_target="tpu_custom_call" | custom-call | tf_op jit(solution)/shard_map/pallas_call | solution.py:283
  33.2 1.1 %shard_map.86 = (bf16[1,256,1280]{2,1,0:T(8,128)(2,1)}, bf16[1,1,512,256]{3,2,1,0:T(8,128)(2,1)}, bf16[1,1,512,256]{3,2,1,0:T(8,128)(2,1)}) custom-call(bf16[256,1280]{1,0:T(8,128)(2,1)S(1)} %get-tuple-element.6.handed_v, bf16[512,256]{1,0:T(8,128)(2,1)S(1)} %get-tuple-element.7.ck_v, bf16[512,256]{1,0:T(8,128)(2,1)S(1)} %get-tuple-element.8.cv_v), custom_call_target="tpu_custom_call" | custom-call | tf_op jit(solution)/shard_map/pallas_call | solution.py:315

commit v2 on v1

v2 whole, which is shorter than its diff:
```python
import functools
import math

import jax
import jax.numpy as jnp
from jax import lax
from jax.experimental import pallas as pl
from jax.experimental.pallas import tpu as pltpu
from jax.sharding import PartitionSpec as P

HEAD = 128
PAGE = 16
NEG = -1e30
MESH = pl.DeviceIdType.MESH


def kernel(
    dims,
    lengths_hbm,
    order_hbm,
    owner_hbm,
    q_hbm,
    k_hbm,
    v_hbm,
    handed,
    ck,
    cv,
    q,
    kall,
    vall,
    mates,
    bias,
    ctx,
    lengths,
    order,
    owner,
    meta_sem,
    in_sem,
    upper_sem,
    next_sem,
    push_send,
    push_recv,
    own_send,
    relay_send,
    recv_sem,
    hand_send,
    hand_recv,
):
    n, sections, cores, tok, kv_heads, width, slots = dims
    pages = tok // PAGE
    me = lax.axis_index("seq")
    sec = lax.axis_index("section")
    core = lax.axis_index("kv")
    onward = lax.rem(sec + 1, sections)
    half = tok // 2
    last = n - 1
    first_core = core == 0

    def head_cols(g):
        return pl.ds(g * HEAD, HEAD)

    def block(t, g, index):
        rows = pl.ds(pl.multiple_of(index * tok, tok), tok)
        return (kall, vall)[t].at[g, rows, pl.ds(0, HEAD)]

    loads = []
    for g in range(kv_heads):
        for t, src in enumerate((k_hbm, v_hbm)):
            load = pltpu.make_async_copy(
                src.at[0, :, head_cols(g)], block(t, g, me), in_sem.at[2 * g + t]
            )
            load.start()
            loads.append(load)
    metas = []
    for src, dst in ((lengths_hbm, lengths), (order_hbm, order), (owner_hbm, owner)):
        metas.append(pltpu.make_async_copy(src, dst, meta_sem.at[len(metas)]))
        metas[-1].start()
    q_load = pltpu.make_async_copy(q_hbm.at[0], q, in_sem.at[2 * kv_heads])
    q_load.start()

    barrier = pltpu.get_barrier_semaphore()
    for c in range(cores):

        @pl.when(core != c)
        def _():
            pl.semaphore_signal(barrier, inc=1, device_id={"kv": c}, device_id_type=MESH)

    below = jnp.where(me > 0, 1, 0) + jnp.where(sec > 0, 1, 0)
    pl.semaphore_wait(barrier, below + (cores - 1))

    @pl.when(me < last)
    def _():
        pl.semaphore_signal(barrier, inc=1, device_id={"seq": me + 1}, device_id_type=MESH)

    @pl.when(sec < sections - 1)
    def _():
        pl.semaphore_signal(barrier, inc=1, device_id={"section": sec + 1}, device_id_type=MESH)

    for j in range(last):

        @pl.when(j < me)
        def _():
            pl.semaphore_signal(
                upper_sem.at[me], inc=1, device_id={"seq": j}, device_id_type=MESH
            )

    @pl.when(sec > 0)
    def _():
        pl.semaphore_signal(next_sem, inc=1, device_id={"section": sec - 1}, device_id_type=MESH)

    units = [(c, g) for g in range(kv_heads) for c in range(cores)]
    inner = (me > 0) & (me < last)

    def gate(j):
        return 1 if j == 0 else n - 2

    def goes(u, j):
        if 0 < j < last:
            return me != j
        straight = me == gate(j)
        if u == 0 and j == 0 and gate(0) != last:
            straight = straight | (me == last)
        return straight

    def relays(g, b):
        found = []
        for j in (0, last):
            if b in (j, gate(j)):
                continue
            cond = me == gate(j)
            if g == 0 and j == 0 and b == last:
                cond = cond & jnp.logical_not(first_core)
            found.append((j, cond))
        return found

    def push(c, g, t):
        return pltpu.make_async_remote_copy(
            src_ref=(k_hbm, v_hbm)[t].at[0, :, head_cols(g)],
            dst_ref=mates.at[c - 1, g, t],
            send_sem=push_send.at[g, t],
            recv_sem=push_recv.at[c - 1, g, t],
            device_id={"kv": 0},
            device_id_type=MESH,
        )

    def own(u, j, t):
        c, g = units[u]
        src = mates.at[c - 1, g, t] if c else (k_hbm, v_hbm)[t].at[0, :, head_cols(g)]
        return pltpu.make_async_remote_copy(
            src_ref=src,
            dst_ref=block(t, g, me),
            send_sem=own_send.at[u, j, t],
            recv_sem=recv_sem.at[g, me, t],
            device_id={"seq": j, "kv": c},
            device_id_type=MESH,
        )

    def relay(g, b, j, t):
        ref = block(t, g, b)
        return pltpu.make_async_remote_copy(
            src_ref=ref,
            dst_ref=ref,
            send_sem=relay_send.at[g, b, t],
            recv_sem=recv_sem.at[g, b, t],
            device_id={"seq": j},
            device_id_type=MESH,
        )

    def send_own(u, j, cond):
        @pl.when(cond & goes(u, j))
        def _():
            for t in range(2):
                own(u, j, t).start()

    downward = sorted(
        ((u, j) for u in range(len(units)) for j in range(last)),
        key=lambda x: (x[0] + max(x[1] - 1, 0), x[1]),
    )
    upward = sorted(
        ((u, j) for u in range(len(units)) for j in range(1, n)),
        key=lambda x: (x[0], -x[1] if x[0] else x[1]),
    )

    @pl.when(jnp.logical_not(first_core))
    def _():
        for c in range(1, cores):

            @pl.when(core == c)
            def _():
                for g in range(kv_heads):
                    for t in range(2):
                        push(c, g, t).start()

    @pl.when(first_core)
    def _():
        here = set()
        for u, j in downward:
            c, g = units[u]
            if c and u not in here:
                here.add(u)
                for t in range(2):
                    push(c, g, t).wait_recv()
            early = (j < me) if u < cores else (j < me) & jnp.logical_not(inner)
            send_own(u, j, early)
        known = set()
        for u, j in upward:
            if j not in known:
                known.add(j)

                @pl.when((j > me) & goes(1, j))
                def _():
                    pl.semaphore_wait(upper_sem.at[j], 1)

            early = (j > me) if u < cores else (j > me) & jnp.logical_not(inner)
            send_own(u, j, early)

    for j in range(1, n):
        unknown = j > me
        unknown = unknown & (jnp.logical_not(first_core) | jnp.logical_not(goes(1, j)))

        @pl.when(unknown)
        def _():
            pl.semaphore_wait(upper_sem.at[j], 1)

    vall[:, :, HEAD:] = jnp.ones((kv_heads, n * tok, HEAD), vall.dtype)
    for meta in metas:
        meta.wait()
    begins = [0]
    for r in range(lengths.shape[1] - 1):
        begins.append(begins[-1] + lengths[0, r])

    def request(position):
        page = position // PAGE
        total = jnp.zeros_like(position)
        for begin in begins[1:]:
            total = total + (page >= begin).astype(jnp.int32)
        return total

    q_pos = order[0, me] * tok + lax.broadcasted_iota(jnp.int32, (tok, 1), 0)
    q_req = request(q_pos)

    def mask(i, _):
        k_pos = order[0, i] * tok + lax.broadcasted_iota(jnp.int32, (1, tok), 1)
        allowed = (request(k_pos) == q_req) & (k_pos <= q_pos)
        bias[:, pl.ds(pl.multiple_of(i * tok, tok), tok)] = jnp.where(allowed, 0.0, NEG)
        return 0

    lax.fori_loop(0, n, mask, 0)
    for load in loads:
        load.wait()
    q_load.wait()

    def pass_on(g, b):
        for j, cond in relays(g, b):

            @pl.when(cond)
            def _():
                for t in range(2):
                    relay(g, b, j, t).wait_recv()
                    relay(g, b, j, t).start()

    hops = {}
    for b in range(n):
        hops.setdefault(min(abs(b - gate(0)), abs(b - gate(last))), []).append(b)
    hops = [hops[d] for d in sorted(hops)]

    def settle(g):
        for b in range(n):
            arrives = me != b
            for _, cond in relays(g, b):
                arrives = arrives & jnp.logical_not(cond)

            @pl.when(arrives)
            def _():
                for t in range(2):
                    relay(g, b, 0, t).wait_recv()

    for blocks in hops:
        for b in blocks:
            pass_on(0, b)

    @pl.when(first_core & inner)
    def _():
        for u, j in downward:
            if u >= cores:
                send_own(u, j, j < me)
        for u, j in upward:
            if u >= cores:
                send_own(u, j, j > me)

    settle(0)

    @pl.when(sec < sections - 1)
    def _():
        pl.semaphore_wait(next_sem, 1)

    factor = math.log2(math.e) / math.sqrt(HEAD)

    def hand(h, part):
        rows = pl.ds(part * half, half)
        cols = pl.ds(pl.multiple_of(h * HEAD, HEAD), HEAD)
        return pltpu.make_async_remote_copy(
            src_ref=ctx.at[rows, cols],
            dst_ref=handed.at[rows, cols],
            send_sem=hand_send.at[h, part],
            recv_sem=hand_recv.at[h, part],
            device_id={"section": onward},
            device_id_type=MESH,
        )

    def heads(g, low, high):
        def one(j, _):
            h = g * width + j
            cols = pl.ds(pl.multiple_of(h * HEAD, HEAD), HEAD)
            for part in range(2):
                rows = pl.ds(part * half, half)
                score = lax.dot_general(
                    q[rows, cols],
                    kall[g],
                    (((1,), (1,)), ((), ())),
                    preferred_element_type=jnp.float32,
                )
                score = score * factor + bias[rows, :]
                top = jnp.max(score, axis=1, keepdims=True)
                weight = jnp.exp2(score - top).astype(jnp.bfloat16)
                mixed = jnp.dot(weight, vall[g], preferred_element_type=jnp.float32)
                ctx[rows, cols] = (mixed[:, :HEAD] / mixed[:, HEAD:]).astype(ctx.dtype)
                hand(h, part).start()
            return 0

        lax.fori_loop(low, high, one, 0)

    taken = slots * PAGE
    lane_page = lax.broadcasted_iota(jnp.int32, (1, tok), 1) // PAGE
    lane_token = lax.broadcasted_iota(jnp.int32, (1, tok), 1) % PAGE

    def keep(g):
        cols = head_cols(g)

        def pick(i, _):
            base = order[0, i] * pages
            target = jnp.full((1, tok), -1, jnp.int32)
            rank = jnp.int32(0)
            for p in range(pages):
                mine = owner[0, base + p] == me
                target = jnp.where(lane_page == p, jnp.where(mine, rank * PAGE, -taken), target)
                rank = rank + mine.astype(jnp.int32)
            target = target + lane_token
            select = lax.broadcasted_iota(jnp.int32, (taken, tok), 0) == target
            select = select.astype(jnp.bfloat16)
            rows = pl.ds(pl.multiple_of(i * tok, tok), tok)
            outs = pl.ds(pl.multiple_of(i * taken, taken), taken)
            for dst, src in ((ck, kall), (cv, vall)):
                dst[outs, cols] = jnp.dot(
                    select, src[g, rows, :HEAD], preferred_element_type=jnp.float32
                ).astype(dst.dtype)
            return 0

        lax.fori_loop(0, n, pick, 0)

    for g in range(kv_heads):
        low = 0
        if g + 1 < kv_heads:
            for i, blocks in enumerate(hops[:-1]):
                cut = (width + 1) // 2 + i * (width // 2) // len(hops)
                heads(g, low, cut)
                low = cut
                for b in blocks:
                    pass_on(g + 1, b)
        heads(g, low, width)
        keep(g)
        if g + 1 < kv_heads:
            for b in hops[-1]:
                pass_on(g + 1, b)
            settle(g + 1)

    for g in range(kv_heads):
        for b in range(n):
            for j, cond in relays(g, b):

                @pl.when(cond)
                def _():
                    for t in range(2):
                        relay(g, b, j, t).wait_send()

    @pl.when(first_core)
    def _():
        for u, j in downward:

            @pl.when((j < me) & goes(u, j))
            def _():
                for t in range(2):
                    own(u, j, t).wait_send()

        for u, j in upward:

            @pl.when((j > me) & goes(u, j))
            def _():
                for t in range(2):
                    own(u, j, t).wait_send()

    for c in range(1, cores):

        @pl.when(core == c)
        def _():
            for g in range(kv_heads):
                for t in range(2):
                    push(c, g, t).wait_send()

    def finish(h, _):
        for part in range(2):
            copy = hand(h, part)
            copy.wait_send()
            copy.wait_recv()
        return 0

    lax.fori_loop(0, kv_heads * width, finish, 0)


def store(handed_v, ck_v, cv_v, handed, ck, cv, sem):
    copies = []
    for src, dst in ((handed_v, handed), (ck_v, ck), (cv_v, cv)):
        rows = src.shape[0] // 2
        view = dst.at[0] if dst.ndim == 3 else dst.at[0, 0]
        for part in range(2):
            piece = pl.ds(part * rows, rows)
            copies.append(
                pltpu.make_async_copy(src.at[piece], view.at[piece], sem.at[len(copies)])
            )
    for copy in copies:
        copy.start()
    for copy in copies:
        copy.wait()


def body(queries, key_rows, values, lengths, block_order, page_owner):
    n, sections = lax.axis_size("seq"), lax.axis_size("section")
    cores = lax.axis_size("kv")
    tok, width = key_rows.shape[1:]
    kv_heads = width // HEAD
    heads = queries.shape[2] // HEAD
    slots = max(2, 2 * (tok // PAGE) // n)
    dims = (n, sections, cores, tok, kv_heads, heads // kv_heads, slots)
    taken = n * slots * PAGE
    dtype = queries.dtype
    metas = lengths, block_order, page_owner.reshape(page_owner.shape[:2])
    vmem = pl.BlockSpec(memory_space=pltpu.VMEM)
    hbm = pl.BlockSpec(memory_space=pltpu.HBM)
    dma = pltpu.SemaphoreType.DMA
    held = pl.pallas_call(
        functools.partial(kernel, dims),
        out_shape=(
            pltpu.VMEM(queries.shape[1:], dtype),
            pltpu.VMEM((taken, width), dtype),
            pltpu.VMEM((taken, width), dtype),
        ),
        in_specs=[hbm] * 6,
        out_specs=(vmem, vmem, vmem),
        scratch_shapes=[
            pltpu.VMEM((tok, heads * HEAD), dtype),
            pltpu.VMEM((kv_heads, n * tok, HEAD), dtype),
            pltpu.VMEM((kv_heads, n * tok, 2 * HEAD), dtype),
            pltpu.VMEM((max(cores - 1, 1), kv_heads, 2, tok, HEAD), dtype),
            pltpu.VMEM((tok, n * tok), jnp.float32),
            pltpu.VMEM((tok, heads * HEAD), dtype),
            *(pltpu.SMEM(x.shape, x.dtype) for x in metas),
            dma((3,)),
            dma((2 * kv_heads + 1,)),
            pltpu.SemaphoreType.REGULAR((n,)),
            pltpu.SemaphoreType.REGULAR,
            dma((kv_heads, 2)),
            dma((max(cores - 1, 1), kv_heads, 2)),
            dma((cores * kv_heads, n, 2)),
            dma((kv_heads, n, 2)),
            dma((kv_heads, n, 2)),
            dma((heads, 2)),
            dma((heads, 2)),
        ],
        compiler_params=pltpu.CompilerParams(
            collective_id=0, has_side_effects=True, vmem_limit_bytes=48 << 20
        ),
    )(
        *(
            pltpu.with_memory_space_constraint(x, pltpu.HBM)
            for x in (*metas, queries, key_rows, values)
        ),
    )
    return pl.pallas_call(
        store,
        out_shape=(
            jax.ShapeDtypeStruct(queries.shape, dtype),
            jax.ShapeDtypeStruct((1, 1, taken, width), dtype),
            jax.ShapeDtypeStruct((1, 1, taken, width), dtype),
        ),
        in_specs=[vmem, vmem, vmem],
        out_specs=(hbm, hbm, hbm),
        scratch_shapes=[dma((6,))],
        compiler_params=pltpu.CompilerParams(vmem_limit_bytes=8 << 20),
    )(*(pltpu.with_memory_space_constraint(x, pltpu.VMEM) for x in held))


def solution(mesh):
    in_specs = (
        P(("groups", "section"), "seq", "kv"),
        P(("groups", "section"), "seq", "kv"),
        P(("groups", "section"), "seq", "kv"),
        P(("groups", "section"), None),
        P(("groups", "section"), None),
        P(("groups", "section"), None, None),
    )
    out_specs = (
        P(("groups", "section"), "seq", "kv"),
        P(("groups", "section"), "seq", None, "kv"),
        P(("groups", "section"), "seq", None, "kv"),
    )
    return jax.shard_map(body, mesh=mesh, in_specs=in_specs, out_specs=out_specs, check_vma=False)
```

time: 34.4 us -> 38 us (1.10)
  the two profiles are of different devices: /device:TPU:0 before, /device:TPU:28 now
where the time goes in v2:
time: 38 us; the launch traced here: 37.9 us
  Pallas kernels  37.3 us (98%)
  between operations  0.64 us (2%)
    pallas_call x1, Pallas kernels, body(): pl.pallas_call(functools.partial(kernel, dims), out_shape=(pltpu.VMEM(que...  36.2 us
    pallas_call x1, Pallas kernels, body(): pl.pallas_call(store, out_shape=(jax.ShapeDtypeStruct(queries.shape, dtyp...  1.06 us

profile of v2, /device:TPU:28, one launch (start us, length us, event | category | flops | bytes accessed | tf_op | source)
XLA Modules:
  0.0 37.9 jit_solution(9233083870148007349)
XLA Ops:
  0.6 36.2 %shard_map.85 = (bf16[256,1280]{1,0:T(8,128)(2,1)S(1)}, bf16[512,256]{1,0:T(8,128)(2,1)S(1)}, bf16[512,256]{1,0:T(8,128)(2,1)S(1)}) custom-call(s32[1,3]{1,0:T(1,128)} %lengths_hbm.1, s32[1,4]{1,0:T(1,128)} %order_hbm.1, s32[1,64]{1,0:T(1,128)} %bitcast.1, bf16[1,256,1280]{2,1,0:T(8,128)(2,1)} %q_hbm.1, bf16[1,256,256]{2,1,0:T(8,128)(2,1)} %k_hbm.1, ...), custom_call_target="tpu_custom_call" | custom-call | tf_op jit(solution)/shard_map/pallas_call | solution.py:450
  36.8 1.1 %shard_map.86 = (bf16[1,256,1280]{2,1,0:T(8,128)(2,1)}, bf16[1,1,512,256]{3,2,1,0:T(8,128)(2,1)}, bf16[1,1,512,256]{3,2,1,0:T(8,128)(2,1)}) custom-call(bf16[256,1280]{1,0:T(8,128)(2,1)S(1)} %get-tuple-element.6.handed_v, bf16[512,256]{1,0:T(8,128)(2,1)S(1)} %get-tuple-element.7.ck_v, bf16[512,256]{1,0:T(8,128)(2,1)S(1)} %get-tuple-element.8.cv_v), custom_call_target="tpu_custom_call" | custom-call | tf_op jit(solution)/shard_map/pallas_call | solution.py:488

commit v3 on v1

--- a/solution.py
+++ b/solution.py
@@ -41,15 +41,20 @@
     in_sem,
     send_sem,
     recv_sem,
+    far_send,
+    upper_sem,
+    next_sem,
     hand_send,
     hand_recv,
 ):
-    n, sections, tok, kv_heads, width, slots = dims
+    n, sections, cores, tok, kv_heads, width, slots = dims
     pages = tok // PAGE
     me = lax.axis_index("seq")
     sec = lax.axis_index("section")
+    core = lax.axis_index("kv")
     right, left = me + 1, me - 1
-    onward, before = lax.rem(sec + 1, sections), lax.rem(sec + sections - 1, sections)
+    onward = lax.rem(sec + 1, sections)
+    straight = n > 2
     half = tok // 2
 
     def block(ref, g, index):
@@ -72,20 +77,19 @@
     q_load.start()
 
     barrier = pltpu.get_barrier_semaphore()
-    others = []
-    if sections > 1:
-        others.append({"section": onward})
-    if sections > 2:
-        others.append({"section": before})
+    below = jnp.where(me > 0, 1, 0) + jnp.where(sec > 0, 1, 0)
+    pl.when(below > 0)(lambda: pl.semaphore_wait(barrier, below))
     pl.when(me < n - 1)(lambda: greet(barrier, {"seq": right}))
-    pl.when(me > 0)(lambda: greet(barrier, {"seq": left}))
-    for peer in others:
-        greet(barrier, peer)
-    beside = jnp.where(me < n - 1, 1, 0) + jnp.where(me > 0, 1, 0)
-    pl.semaphore_wait(barrier, beside + len(others))
-
-    def sends(way, d):
-        return (me < n - 1) & (me >= d - 1) if way == 0 else (me > 0) & (me <= n - d)
+    pl.when(sec < sections - 1)(lambda: greet(barrier, {"section": sec + 1}))
+    pl.when(me > 0)(lambda: greet(upper_sem, {"seq": left}))
+    pl.when(sec > 0)(lambda: greet(next_sem, {"section": sec - 1}))
+
+    def sends(way, g, d):
+        if way == 0:
+            return (me < n - 1) & (me >= d - 1)
+        if straight and g == 0 and d == n - 1:
+            return me < 0
+        return (me > 0) & (me <= n - d)
 
     def takes(way, d):
         return me >= d if way == 0 else me + d <= n - 1
@@ -93,8 +97,11 @@
     def line(way, g, d, t, arriving):
         shift = d if arriving else d - 1
         ref = block((kall, vall)[t], g, me - shift if way == 0 else me + shift)
+        src = ref
+        if d == 1 and not arriving:
+            src = (k_hbm, v_hbm)[t].at[0, :, pl.ds(g * HEAD, HEAD)]
         return pltpu.make_async_remote_copy(
-            src_ref=ref,
+            src_ref=src,
             dst_ref=ref,
             send_sem=send_sem.at[way, g, d - 1, t],
             recv_sem=recv_sem.at[way, g, d - 1, t],
@@ -102,16 +109,25 @@
             device_id_type=MESH,
         )
 
-    def start(g, ts=(0, 1)):
+    def far(t):
+        return pltpu.make_async_remote_copy(
+            src_ref=(k_hbm, v_hbm)[t].at[0, :, pl.ds(0, HEAD)],
+            dst_ref=block((kall, vall)[t], 0, me),
+            send_sem=far_send.at[t],
+            recv_sem=recv_sem.at[1, 0, n - 2, t],
+            device_id={"seq": 0},
+            device_id_type=MESH,
+        )
+
+    def start(way, g, ts=(0, 1)):
         for t in ts:
-            for way in range(2):
-                pl.when(sends(way, 1))(lambda: line(way, g, 1, t, False).start())
+            pl.when(sends(way, g, 1))(lambda: line(way, g, 1, t, False).start())
 
     def pass_on(g, d):
         for t in range(2):
             for way in range(2):
 
-                @pl.when(sends(way, d + 1))
+                @pl.when(sends(way, g, d + 1))
                 def _():
                     line(way, g, d, t, True).wait_recv()
                     line(way, g, d + 1, t, False).start()
@@ -120,16 +136,19 @@
         for d in range(1, n):
             for t in range(2):
                 for way in range(2):
-                    ends = takes(way, d) & jnp.logical_not(sends(way, d + 1))
+                    ends = takes(way, d) & jnp.logical_not(sends(way, g, d + 1))
                     pl.when(ends)(lambda: line(way, g, d, t, True).wait_recv())
 
-    loads[0].wait()
-    loads[1].wait()
-    start(0)
-    for load in loads[2:]:
-        load.wait()
+    if straight:
+        for t in range(2):
+            pl.when(me == n - 1)(lambda: far(t).start())
+    start(1, 0)
     for g in range(1, kv_heads):
-        start(g, (0,))
+        start(1, g, (0,))
+    pl.when(me < n - 1)(lambda: pl.semaphore_wait(upper_sem, 1))
+    start(0, 0)
+    for g in range(1, kv_heads):
+        start(0, g, (0,))
 
     vall[:, :, HEAD:] = jnp.ones((kv_heads, n * tok, HEAD), vall.dtype)
     for meta in metas:
@@ -155,12 +174,16 @@
         return 0
 
     lax.fori_loop(0, n, mask, 0)
-    q_load.wait()
 
     for d in range(1, n - 1):
         pass_on(0, d)
     for g in range(1, kv_heads):
-        start(g, (1,))
+        for way in range(2):
+            start(way, g, (1,))
+    for load in loads:
+        load.wait()
+    q_load.wait()
+    pl.when(sec < sections - 1)(lambda: pl.semaphore_wait(next_sem, 1))
     settle(0)
 
     factor = math.log2(math.e) / math.sqrt(HEAD)
@@ -177,11 +200,10 @@
         )
 
     def heads(g, low, high):
-        def one(j, _):
-            h = g * width + j
-            cols = pl.ds(pl.multiple_of(h * HEAD, HEAD), HEAD)
-            for part in range(2):
-                rows = pl.ds(part * half, half)
+        for part in range(2):
+            rows = pl.ds(part * half, half)
+            for h in range(g * width + low, g * width + high):
+                cols = pl.ds(h * HEAD, HEAD)
                 score = lax.dot_general(
                     q[rows, cols],
                     kall[g],
@@ -193,10 +215,8 @@
                 weight = jnp.exp2(score - top).astype(jnp.bfloat16)
                 mixed = jnp.dot(weight, vall[g], preferred_element_type=jnp.float32)
                 ctx[rows, cols] = (mixed[:, :HEAD] / mixed[:, HEAD:]).astype(ctx.dtype)
+        for h in range(g * width + low, g * width + high):
             hand(h).start()
-            return 0
-
-        lax.fori_loop(low, high, one, 0)
 
     for g in range(kv_heads):
         last = g + 1 == kv_heads
@@ -239,7 +259,11 @@
         for d in range(1, n):
             for t in range(2):
                 for way in range(2):
-                    pl.when(sends(way, d))(lambda: line(way, g, d, t, False).wait_send())
+                    pl.when(sends(way, g, d))(lambda: line(way, g, d, t, False).wait_send())
+
+    if straight:
+        for t in range(2):
+            pl.when(me == n - 1)(lambda: far(t).wait_send())
 
     def finish(h, _):
         copy = hand(h)
@@ -272,7 +296,8 @@
     kv_heads = key_rows.shape[2] // HEAD
     heads = queries.shape[2] // HEAD
     slots = max(2, 2 * (tok // PAGE) // n)
-    dims = (n, sections, tok, kv_heads, heads // kv_heads, slots)
+    cores = lax.axis_size("kv")
+    dims = (n, sections, cores, tok, kv_heads, heads // kv_heads, slots)
     steps = max(n - 1, 1)
     taken = n * slots * PAGE
     dtype = queries.dtype
@@ -300,6 +325,9 @@
             pltpu.SemaphoreType.DMA((2 * kv_heads + 1,)),
             pltpu.SemaphoreType.DMA((2, kv_heads, steps, 2)),
             pltpu.SemaphoreType.DMA((2, kv_heads, steps, 2)),
+            pltpu.SemaphoreType.DMA((2,)),
+            pltpu.SemaphoreType.REGULAR,
+            pltpu.SemaphoreType.REGULAR,
             pltpu.SemaphoreType.DMA((heads,)),
             pltpu.SemaphoreType.DMA((heads,)),
         ],

time: 34.4 us -> 33.6 us (0.977)
  Pallas kernels: 33.6 us -> 32.8 us
    pallas_call x1, Pallas kernels: 32.6 us -> 31.8 us  [body(): pl.pallas_call(functools.partial(kernel, dims), out_shape=(pltpu.VMEM(que...]
where the time goes in v3:
time: 33.6 us; the launch traced here: 33.5 us
  Pallas kernels  32.8 us (98%)
  between operations  0.64 us (2%)
    pallas_call x1, Pallas kernels, body(): pl.pallas_call(functools.partial(kernel, dims), out_shape=(pltpu.VMEM(que...  31.8 us
    pallas_call x1, Pallas kernels, body(): pl.pallas_call(store, out_shape=(jax.ShapeDtypeStruct(queries.shape, dtyp...  1.06 us

profile of v3, /device:TPU:0, one launch (start us, length us, event | category | flops | bytes accessed | tf_op | source)
XLA Modules:
  0.0 33.5 jit_solution(645288466266715155)
XLA Ops:
  0.6 31.8 %shard_map.85 = (bf16[256,1280]{1,0:T(8,128)(2,1)S(1)}, bf16[512,256]{1,0:T(8,128)(2,1)S(1)}, bf16[512,256]{1,0:T(8,128)(2,1)S(1)}) custom-call(s32[1,3]{1,0:T(1,128)} %lengths_hbm.1, s32[1,4]{1,0:T(1,128)} %order_hbm.1, s32[1,64]{1,0:T(1,128)} %bitcast.1, bf16[1,256,1280]{2,1,0:T(8,128)(2,1)} %q_hbm.1, bf16[1,256,256]{2,1,0:T(8,128)(2,1)} %k_hbm.1, ...), custom_call_target="tpu_custom_call" | custom-call | tf_op jit(solution)/shard_map/pallas_call | solution.py:308
  32.4 1.1 %shard_map.86 = (bf16[1,256,1280]{2,1,0:T(8,128)(2,1)}, bf16[1,1,512,256]{3,2,1,0:T(8,128)(2,1)}, bf16[1,1,512,256]{3,2,1,0:T(8,128)(2,1)}) custom-call(bf16[256,1280]{1,0:T(8,128)(2,1)S(1)} %get-tuple-element.6.handed_v, bf16[512,256]{1,0:T(8,128)(2,1)S(1)} %get-tuple-element.7.ck_v, bf16[512,256]{1,0:T(8,128)(2,1)S(1)} %get-tuple-element.8.cv_v), custom_call_target="tpu_custom_call" | custom-call | tf_op jit(solution)/shard_map/pallas_call | solution.py:343

commit v4 on v3

--- a/solution.py
+++ b/solution.py
@@ -33,6 +33,7 @@
     kall,
     vall,
     bias,
+    weights,
     ctx,
     lengths,
     order,
@@ -132,12 +133,11 @@
                     line(way, g, d, t, True).wait_recv()
                     line(way, g, d + 1, t, False).start()
 
-    def settle(g):
+    def settle(g, t):
         for d in range(1, n):
-            for t in range(2):
-                for way in range(2):
-                    ends = takes(way, d) & jnp.logical_not(sends(way, g, d + 1))
-                    pl.when(ends)(lambda: line(way, g, d, t, True).wait_recv())
+            for way in range(2):
+                ends = takes(way, d) & jnp.logical_not(sends(way, g, d + 1))
+                pl.when(ends)(lambda: line(way, g, d, t, True).wait_recv())
 
     if straight:
         for t in range(2):
@@ -184,7 +184,6 @@
         load.wait()
     q_load.wait()
     pl.when(sec < sections - 1)(lambda: pl.semaphore_wait(next_sem, 1))
-    settle(0)
 
     factor = math.log2(math.e) / math.sqrt(HEAD)
 
@@ -199,23 +198,39 @@
             device_id_type=MESH,
         )
 
+    def weigh(g, h, rows):
+        score = lax.dot_general(
+            q[rows, pl.ds(h * HEAD, HEAD)],
+            kall[g],
+            (((1,), (1,)), ((), ())),
+            preferred_element_type=jnp.float32,
+        )
+        score = score * factor + bias[rows, :]
+        top = jnp.max(score, axis=1, keepdims=True)
+        return jnp.exp2(score - top).astype(jnp.bfloat16)
+
+    def mix(g, h, rows, weight):
+        mixed = jnp.dot(weight, vall[g], preferred_element_type=jnp.float32)
+        mixed = mixed[:, :HEAD] / mixed[:, HEAD:]
+        ctx[rows, pl.ds(h * HEAD, HEAD)] = mixed.astype(ctx.dtype)
+
     def heads(g, low, high):
-        for part in range(2):
-            rows = pl.ds(part * half, half)
-            for h in range(g * width + low, g * width + high):
-                cols = pl.ds(h * HEAD, HEAD)
-                score = lax.dot_general(
-                    q[rows, cols],
-                    kall[g],
-                    (((1,), (1,)), ((), ())),
-                    preferred_element_type=jnp.float32,
-                )
-                score = score * factor + bias[rows, :]
-                top = jnp.max(score, axis=1, keepdims=True)
-                weight = jnp.exp2(score - top).astype(jnp.bfloat16)
-                mixed = jnp.dot(weight, vall[g], preferred_element_type=jnp.float32)
-                ctx[rows, cols] = (mixed[:, :HEAD] / mixed[:, HEAD:]).astype(ctx.dtype)
-        for h in range(g * width + low, g * width + high):
+        several = range(g * width + low, g * width + high)
+        halves = [pl.ds(part * half, half) for part in range(2)]
+        if low == 0:
+            settle(g, 0)
+            for rows in halves:
+                for i, h in enumerate(several):
+                    weights[i, rows, :] = weigh(g, h, rows)
+            settle(g, 1)
+            for rows in halves:
+                for i, h in enumerate(several):
+                    mix(g, h, rows, weights[i, rows, :])
+        else:
+            for rows in halves:
+                for h in several:
+                    mix(g, h, rows, weigh(g, h, rows))
+        for h in several:
             hand(h).start()
 
     for g in range(kv_heads):
@@ -228,7 +243,6 @@
         if not last:
             for d in range((width - 1) // 2 + 1, n - 1):
                 pass_on(g + 1, d)
-            settle(g + 1)
 
     taken = slots * PAGE
     lane_page = lax.broadcasted_iota(jnp.int32, (1, tok), 1) // PAGE
@@ -277,9 +291,9 @@
 def store(handed_v, ck_v, cv_v, handed, ck, cv, sem):
     copies = []
     for src, dst in ((handed_v, handed), (ck_v, ck), (cv_v, cv)):
-        rows = src.shape[0] // 2
+        rows = src.shape[0] // 4
         view = dst.at[0] if dst.ndim == 3 else dst.at[0, 0]
-        for part in range(2):
+        for part in range(4):
             piece = pl.ds(part * rows, rows)
             copies.append(
                 pltpu.make_async_copy(src.at[piece], view.at[piece], sem.at[len(copies)])
@@ -319,6 +333,7 @@
             pltpu.VMEM((kv_heads, n * tok, HEAD), dtype),
             pltpu.VMEM((kv_heads, n * tok, 2 * HEAD), dtype),
             pltpu.VMEM((tok, n * tok), jnp.float32),
+            pltpu.VMEM((2, tok, n * tok), dtype),
             pltpu.VMEM((tok, heads * HEAD), dtype),
             *(pltpu.SMEM(x.shape, x.dtype) for x in metas),
             pltpu.SemaphoreType.DMA((3,)),
@@ -349,7 +364,7 @@
         ),
         in_specs=[vmem, vmem, vmem],
         out_specs=(hbm, hbm, hbm),
-        scratch_shapes=[pltpu.SemaphoreType.DMA((6,))],
+        scratch_shapes=[pltpu.SemaphoreType.DMA((12,))],
         compiler_params=pltpu.CompilerParams(vmem_limit_bytes=8 << 20),
     )(*(pltpu.with_memory_space_constraint(x, pltpu.VMEM) for x in held))
 

time: 33.6 us -> 32.4 us (0.964)
  Pallas kernels: 32.8 us -> 31.6 us
    pallas_call x1, Pallas kernels: 31.8 us -> 30.5 us  [body(): pl.pallas_call(functools.partial(kernel, dims), out_shape=(pltpu.VMEM(que...]
where the time goes in v4:
time: 32.4 us; the launch traced here: 32.3 us
  Pallas kernels  31.6 us (98%)
  between operations  0.64 us (2%)
    pallas_call x1, Pallas kernels, body(): pl.pallas_call(functools.partial(kernel, dims), out_shape=(pltpu.VMEM(que...  30.5 us
    pallas_call x1, Pallas kernels, body(): pl.pallas_call(store, out_shape=(jax.ShapeDtypeStruct(queries.shape, dtyp...  1.1 us

profile of v4, /device:TPU:0, one launch (start us, length us, event | category | flops | bytes accessed | tf_op | source)
XLA Modules:
  0.0 32.3 jit_solution(14928109601548993175)
XLA Ops:
  0.6 30.5 %shard_map.85 = (bf16[256,1280]{1,0:T(8,128)(2,1)S(1)}, bf16[512,256]{1,0:T(8,128)(2,1)S(1)}, bf16[512,256]{1,0:T(8,128)(2,1)S(1)}) custom-call(s32[1,3]{1,0:T(1,128)} %lengths_hbm.1, s32[1,4]{1,0:T(1,128)} %order_hbm.1, s32[1,64]{1,0:T(1,128)} %bitcast.1, bf16[1,256,1280]{2,1,0:T(8,128)(2,1)} %q_hbm.1, bf16[1,256,256]{2,1,0:T(8,128)(2,1)} %k_hbm.1, ...), custom_call_target="tpu_custom_call" | custom-call | tf_op jit(solution)/shard_map/pallas_call | solution.py:322
  31.2 1.1 %shard_map.86 = (bf16[1,256,1280]{2,1,0:T(8,128)(2,1)}, bf16[1,1,512,256]{3,2,1,0:T(8,128)(2,1)}, bf16[1,1,512,256]{3,2,1,0:T(8,128)(2,1)}) custom-call(bf16[256,1280]{1,0:T(8,128)(2,1)S(1)} %get-tuple-element.6.handed_v, bf16[512,256]{1,0:T(8,128)(2,1)S(1)} %get-tuple-element.7.ck_v, bf16[512,256]{1,0:T(8,128)(2,1)S(1)} %get-tuple-element.8.cv_v), custom_call_target="tpu_custom_call" | custom-call | tf_op jit(solution)/shard_map/pallas_call | solution.py:358

commit v5 on v4

--- a/solution.py
+++ b/solution.py
@@ -62,6 +62,74 @@
         rows = pl.ds(pl.multiple_of(index * tok, tok), tok)
         return ref.at[g, rows, pl.ds(0, HEAD)]
 
+    barrier = pltpu.get_barrier_semaphore()
+    below = jnp.where(me > 0, 1, 0) + jnp.where(sec > 0, 1, 0)
+    pl.when(below > 0)(lambda: pl.semaphore_wait(barrier, below))
+    pl.when(me < n - 1)(lambda: greet(barrier, {"seq": right}))
+    pl.when(sec < sections - 1)(lambda: greet(barrier, {"section": sec + 1}))
+    pl.when(me > 0)(lambda: greet(upper_sem, {"seq": left}))
+    pl.when(sec > 0)(lambda: greet(next_sem, {"section": sec - 1}))
+
+    def sends(way, g, d):
+        if way == 0:
+            return (me < n - 1) & (me >= d - 1)
+        if straight and g == 0 and d == n - 1:
+            return me < 0
+        return (me > 0) & (me <= n - d)
+
+    def takes(way, d):
+        return me >= d if way == 0 else me + d <= n - 1
+
+    def line(way, g, d, t, arriving):
+        shift = d if arriving else d - 1
+        ref = block((kall, vall)[t], g, me - shift if way == 0 else me + shift)
+        src = ref
+        if d == 1 and not arriving:
+            src = (k_hbm, v_hbm)[t].at[0, :, pl.ds(g * HEAD, HEAD)]
+        return pltpu.make_async_remote_copy(
+            src_ref=src,
+            dst_ref=ref,
+            send_sem=send_sem.at[way, g, d - 1, t],
+            recv_sem=recv_sem.at[way, g, d - 1, t],
+            device_id={"seq": right if way == 0 else left},
+            device_id_type=MESH,
+        )
+
+    def far(t):
+        return pltpu.make_async_remote_copy(
+            src_ref=(k_hbm, v_hbm)[t].at[0, :, pl.ds(0, HEAD)],
+            dst_ref=block((kall, vall)[t], 0, me),
+            send_sem=far_send.at[t],
+            recv_sem=recv_sem.at[1, 0, n - 2, t],
+            device_id={"seq": 0},
+            device_id_type=MESH,
+        )
+
+    def start(way, g, ts=(0, 1)):
+        for t in ts:
+            pl.when(sends(way, g, 1))(lambda: line(way, g, 1, t, False).start())
+
+    def pass_on(g, d):
+        for t in range(2):
+            for way in range(2):
+
+                @pl.when(sends(way, g, d + 1))
+                def _():
+                    line(way, g, d, t, True).wait_recv()
+                    line(way, g, d + 1, t, False).start()
+
+    def settle(g, t):
+        for d in range(1, n):
+            for way in range(2):
+                ends = takes(way, d) & jnp.logical_not(sends(way, g, d + 1))
+                pl.when(ends)(lambda: line(way, g, d, t, True).wait_recv())
+
+    if straight:
+        for t in range(2):
+            pl.when(me == n - 1)(lambda: far(t).start())
+    start(1, 0)
+    for g in range(1, kv_heads):
+        start(1, g, (0,))
     loads = []
     for g in range(kv_heads):
         for t, (src, dst) in enumerate(((k_hbm, kall), (v_hbm, vall))):
@@ -77,74 +145,6 @@
     q_load = pltpu.make_async_copy(q_hbm.at[0], q, in_sem.at[2 * kv_heads])
     q_load.start()
 
-    barrier = pltpu.get_barrier_semaphore()
-    below = jnp.where(me > 0, 1, 0) + jnp.where(sec > 0, 1, 0)
-    pl.when(below > 0)(lambda: pl.semaphore_wait(barrier, below))
-    pl.when(me < n - 1)(lambda: greet(barrier, {"seq": right}))
-    pl.when(sec < sections - 1)(lambda: greet(barrier, {"section": sec + 1}))
-    pl.when(me > 0)(lambda: greet(upper_sem, {"seq": left}))
-    pl.when(sec > 0)(lambda: greet(next_sem, {"section": sec - 1}))
-
-    def sends(way, g, d):
-        if way == 0:
-            return (me < n - 1) & (me >= d - 1)
-        if straight and g == 0 and d == n - 1:
-            return me < 0
-        return (me > 0) & (me <= n - d)
-
-    def takes(way, d):
-        return me >= d if way == 0 else me + d <= n - 1
-
-    def line(way, g, d, t, arriving):
-        shift = d if arriving else d - 1
-        ref = block((kall, vall)[t], g, me - shift if way == 0 else me + shift)
-        src = ref
-        if d == 1 and not arriving:
-            src = (k_hbm, v_hbm)[t].at[0, :, pl.ds(g * HEAD, HEAD)]
-        return pltpu.make_async_remote_copy(
-            src_ref=src,
-            dst_ref=ref,
-            send_sem=send_sem.at[way, g, d - 1, t],
-            recv_sem=recv_sem.at[way, g, d - 1, t],
-            device_id={"seq": right if way == 0 else left},
-            device_id_type=MESH,
-        )
-
-    def far(t):
-        return pltpu.make_async_remote_copy(
-            src_ref=(k_hbm, v_hbm)[t].at[0, :, pl.ds(0, HEAD)],
-            dst_ref=block((kall, vall)[t], 0, me),
-            send_sem=far_send.at[t],
-            recv_sem=recv_sem.at[1, 0, n - 2, t],
-            device_id={"seq": 0},
-            device_id_type=MESH,
-        )
-
-    def start(way, g, ts=(0, 1)):
-        for t in ts:
-            pl.when(sends(way, g, 1))(lambda: line(way, g, 1, t, False).start())
-
-    def pass_on(g, d):
-        for t in range(2):
-            for way in range(2):
-
-                @pl.when(sends(way, g, d + 1))
-                def _():
-                    line(way, g, d, t, True).wait_recv()
-                    line(way, g, d + 1, t, False).start()
-
-    def settle(g, t):
-        for d in range(1, n):
-            for way in range(2):
-                ends = takes(way, d) & jnp.logical_not(sends(way, g, d + 1))
-                pl.when(ends)(lambda: line(way, g, d, t, True).wait_recv())
-
-    if straight:
-        for t in range(2):
-            pl.when(me == n - 1)(lambda: far(t).start())
-    start(1, 0)
-    for g in range(1, kv_heads):
-        start(1, g, (0,))
     pl.when(me < n - 1)(lambda: pl.semaphore_wait(upper_sem, 1))
     start(0, 0)
     for g in range(1, kv_heads):
@@ -223,15 +223,16 @@
                 for i, h in enumerate(several):
                     weights[i, rows, :] = weigh(g, h, rows)
             settle(g, 1)
-            for rows in halves:
-                for i, h in enumerate(several):
+            for i, h in enumerate(several):
+                for rows in halves:
                     mix(g, h, rows, weights[i, rows, :])
+                hand(h).start()
         else:
             for rows in halves:
                 for h in several:
                     mix(g, h, rows, weigh(g, h, rows))
-        for h in several:
-            hand(h).start()
+            for h in several:
+                hand(h).start()
 
     for g in range(kv_heads):
         last = g + 1 == kv_heads

time: 32.4 us -> 32.3 us (level)
  no operation moved by 1% of the time
where the time goes in v5:
time: 32.3 us; the launch traced here: 32.2 us
  Pallas kernels  31.5 us (98%)
  between operations  0.64 us (2%)
    pallas_call x1, Pallas kernels, body(): pl.pallas_call(functools.partial(kernel, dims), out_shape=(pltpu.VMEM(que...  30.4 us
    pallas_call x1, Pallas kernels, body(): pl.pallas_call(store, out_shape=(jax.ShapeDtypeStruct(queries.shape, dtyp...  1.1 us

profile of v5, /device:TPU:0, one launch (start us, length us, event | category | flops | bytes accessed | tf_op | source)
XLA Modules:
  0.0 32.2 jit_solution(4920749756328579893)
XLA Ops:
  0.6 30.4 %shard_map.85 = (bf16[256,1280]{1,0:T(8,128)(2,1)S(1)}, bf16[512,256]{1,0:T(8,128)(2,1)S(1)}, bf16[512,256]{1,0:T(8,128)(2,1)S(1)}) custom-call(s32[1,3]{1,0:T(1,128)} %lengths_hbm.1, s32[1,4]{1,0:T(1,128)} %order_hbm.1, s32[1,64]{1,0:T(1,128)} %bitcast.1, bf16[1,256,1280]{2,1,0:T(8,128)(2,1)} %q_hbm.1, bf16[1,256,256]{2,1,0:T(8,128)(2,1)} %k_hbm.1, ...), custom_call_target="tpu_custom_call" | custom-call | tf_op jit(solution)/shard_map/pallas_call | solution.py:323
  31.1 1.1 %shard_map.86 = (bf16[1,256,1280]{2,1,0:T(8,128)(2,1)}, bf16[1,1,512,256]{3,2,1,0:T(8,128)(2,1)}, bf16[1,1,512,256]{3,2,1,0:T(8,128)(2,1)}) custom-call(bf16[256,1280]{1,0:T(8,128)(2,1)S(1)} %get-tuple-element.6.handed_v, bf16[512,256]{1,0:T(8,128)(2,1)S(1)} %get-tuple-element.7.ck_v, bf16[512,256]{1,0:T(8,128)(2,1)S(1)} %get-tuple-element.8.cv_v), custom_call_target="tpu_custom_call" | custom-call | tf_op jit(solution)/shard_map/pallas_call | solution.py:359

commit v6 on v5

--- a/solution.py
+++ b/solution.py
@@ -124,10 +124,10 @@
                 ends = takes(way, d) & jnp.logical_not(sends(way, g, d + 1))
                 pl.when(ends)(lambda: line(way, g, d, t, True).wait_recv())
 
-    if straight:
-        for t in range(2):
+    for t in range(2):
+        if straight:
             pl.when(me == n - 1)(lambda: far(t).start())
-    start(1, 0)
+        start(1, 0, (t,))
     for g in range(1, kv_heads):
         start(1, g, (0,))
     loads = []

time: 32.3 us -> 32.3 us (level)
  no operation moved by 1% of the time
where the time goes in v6:
time: 32.3 us; the launch traced here: 32.2 us
  Pallas kernels  31.6 us (98%)
  between operations  0.64 us (2%)
    pallas_call x1, Pallas kernels, body(): pl.pallas_call(functools.partial(kernel, dims), out_shape=(pltpu.VMEM(que...  30.5 us
    pallas_call x1, Pallas kernels, body(): pl.pallas_call(store, out_shape=(jax.ShapeDtypeStruct(queries.shape, dtyp...  1.1 us

profile of v6, /device:TPU:0, one launch (start us, length us, event | category | flops | bytes accessed | tf_op | source)
XLA Modules:
  0.0 32.2 jit_solution(7997682820876153832)
XLA Ops:
  0.6 30.5 %shard_map.85 = (bf16[256,1280]{1,0:T(8,128)(2,1)S(1)}, bf16[512,256]{1,0:T(8,128)(2,1)S(1)}, bf16[512,256]{1,0:T(8,128)(2,1)S(1)}) custom-call(s32[1,3]{1,0:T(1,128)} %lengths_hbm.1, s32[1,4]{1,0:T(1,128)} %order_hbm.1, s32[1,64]{1,0:T(1,128)} %bitcast.1, bf16[1,256,1280]{2,1,0:T(8,128)(2,1)} %q_hbm.1, bf16[1,256,256]{2,1,0:T(8,128)(2,1)} %k_hbm.1, ...), custom_call_target="tpu_custom_call" | custom-call | tf_op jit(solution)/shard_map/pallas_call | solution.py:323
  31.1 1.1 %shard_map.86 = (bf16[1,256,1280]{2,1,0:T(8,128)(2,1)}, bf16[1,1,512,256]{3,2,1,0:T(8,128)(2,1)}, bf16[1,1,512,256]{3,2,1,0:T(8,128)(2,1)}) custom-call(bf16[256,1280]{1,0:T(8,128)(2,1)S(1)} %get-tuple-element.6.handed_v, bf16[512,256]{1,0:T(8,128)(2,1)S(1)} %get-tuple-element.7.ck_v, bf16[512,256]{1,0:T(8,128)(2,1)S(1)} %get-tuple-element.8.cv_v), custom_call_target="tpu_custom_call" | custom-call | tf_op jit(solution)/shard_map/pallas_call | solution.py:359
